TPU v7x, 256 devices: a whole 4x4x8 slice. The times are simulated.
256 devices in a mesh: dp: 8 (over z), expert: 32 (over x, y, core).
Axes of the slice: x: 4, y: 4, z: 8, core: 2. Of those that a mesh axis runs over, the one named last changes fastest.
Arguments:
- tokens: bfloat16 [16384, 2048], P(('dp', 'expert')), may hold values from -6 to 6
- norm_gain: bfloat16 [2048], replicated, may hold values from 0.099609375 to 1.8984375
- router_weight: bfloat16 [2048, 32], replicated, may hold values from -0.125 to 0.125
- gate_weight: bfloat16 [32, 2048, 5120], P('expert', None, 'dp'), may hold values from -0.125 to 0.125
- up_weight: bfloat16 [32, 2048, 5120], P('expert', None, 'dp'), may hold values from -0.125 to 0.125
- down_weight: bfloat16 [32, 5120, 2048], P('expert', 'dp'), may hold values from -0.078125 to 0.078125
- expert_picks: int32 [8, 32, 128], P('dp'), may hold values from 0 to 2047, as said below
- final_gain: bfloat16 [2048], replicated, may hold values from 0.099609375 to 1.8984375
- kv_weight: bfloat16 [2048, 32, 6, 2, 64], P(None, 'expert'), may hold values from -0.125 to 0.125
Outputs:
- moe_out: bfloat16 [16384, 2048], P(('dp', 'expert'))
- kv_cache: bfloat16 [16384, 32, 6, 2, 64], P('dp', 'expert')
Inputs may be any that keep to these rules, and one draw needn't show every extreme that they name: `expert_picks`: for each group and expert, 128 different positions in the group. Of the 64 tokens of one device (positions s * 64 to (s + 1) * 64 - 1) one expert picks at most 8, and for every group and expert some device's tokens are picked exactly 8 times.
All inputs are finite; a program needn't handle non-finite values.
Results may differ from a plain program's by a relative error of at most 0.013.
Values may be sent and summed in bfloat16 or wider, within the bound.
A program may use at most 128 MiB of HBM per device.

v0:
```python
import jax
import jax.numpy as jnp
from jax import lax
from jax.sharding import PartitionSpec as P


def normalize(values, gain):
    return (
        values
        * lax.rsqrt(jnp.mean(values * values, axis=-1, keepdims=True) + 1e-06)
        * gain.astype(jnp.float32)
    )


def local(
    tokens,
    norm_gain,
    router_weight,
    gate_weight,
    up_weight,
    down_weight,
    expert_picks,
    final_gain,
    kv_weight,
):
    expert_count = lax.axis_size("expert")
    own_index = lax.axis_index("expert")
    tok_rows = tokens.shape[0]
    wide_tokens = tokens.astype(jnp.float32)
    normed = normalize(wide_tokens, norm_gain).astype(jnp.bfloat16)
    gate_probs = jax.nn.sigmoid(jnp.dot(normed, router_weight, preferred_element_type=jnp.float32))
    chosen = expert_picks[0]
    capacity = chosen.shape[1]
    slot_count = 4 * tok_rows // expert_count
    source = chosen // tok_rows
    local_row = chosen % tok_rows
    positions = jnp.arange(capacity, dtype=jnp.int32)
    earlier = (source[:, :, None] == source[:, None, :]) & (
        positions[None, None, :] < positions[None, :, None]
    )
    slot_rank = jnp.sum(earlier.astype(jnp.int32), axis=2)
    slot_ids = jnp.arange(slot_count, dtype=jnp.int32)
    shard_ids = jnp.arange(expert_count, dtype=jnp.int32)
    own_source = lax.dynamic_index_in_dim(source, own_index, 0, keepdims=False)
    own_rank = lax.dynamic_index_in_dim(slot_rank, own_index, 0, keepdims=False)
    compact_map = (
        (own_source[:, None, None] == shard_ids[None, :, None])
        & (own_rank[:, None, None] == slot_ids[None, None, :])
    ).astype(jnp.bfloat16)
    send_slot = (
        (source == own_index)[:, :, None] & (slot_rank[:, :, None] == slot_ids[None, None, :])
    ).astype(jnp.bfloat16)
    local_map = (
        local_row[:, :, None] == jnp.arange(tok_rows, dtype=jnp.int32)[None, None, :]
    ).astype(jnp.bfloat16)
    send_map = jnp.einsum("ecm,ect->emt", send_slot, local_map, preferred_element_type=jnp.float32)
    outgoing = jnp.einsum(
        "emt,td->emd", send_map.astype(jnp.bfloat16), normed, preferred_element_type=jnp.float32
    ).astype(jnp.bfloat16)
    incoming = lax.all_to_all(outgoing, "expert", split_axis=0, concat_axis=0, tiled=True)
    picked = jnp.einsum(
        "csm,smd->cd", compact_map, incoming, preferred_element_type=jnp.float32
    ).astype(jnp.bfloat16)
    gate_proj = gate_weight[0]
    up_proj = up_weight[0]
    down_proj = down_weight[0]
    block_rows = lax.all_gather(picked, "dp", axis=0, tiled=True)
    gate_act = jnp.dot(block_rows, gate_proj, preferred_element_type=jnp.float32)
    up_act = jnp.dot(block_rows, up_proj, preferred_element_type=jnp.float32)
    hidden_all = (jax.nn.gelu(gate_act, approximate=True) * up_act).astype(jnp.bfloat16)
    summed = lax.psum_scatter(
        jnp.dot(hidden_all, down_proj, preferred_element_type=jnp.float32).astype(jnp.bfloat16),
        "dp",
        scatter_dimension=0,
        tiled=True,
    )
    outbound = jnp.einsum(
        "csm,cd->smd", compact_map, summed, preferred_element_type=jnp.float32
    ).astype(jnp.bfloat16)
    returned = lax.all_to_all(outbound, "expert", split_axis=0, concat_axis=0, tiled=True)
    combine_weight = jnp.transpose(send_map, (2, 0, 1)) * gate_probs[:, :, None]
    combined = jnp.einsum("tem,emd->td", combine_weight, returned.astype(jnp.float32))
    moe_out = (wide_tokens + combined).astype(jnp.bfloat16)
    encoded = normalize(moe_out.astype(jnp.float32), final_gain).astype(jnp.bfloat16)
    kv_matrix = kv_weight.reshape(kv_weight.shape[0], -1)
    kv_rows = jnp.dot(
        lax.all_gather(encoded, "expert", axis=0, tiled=True),
        kv_matrix,
        preferred_element_type=jnp.float32,
    ).astype(jnp.bfloat16)
    kv_cache = kv_rows.reshape((kv_rows.shape[0],) + kv_weight.shape[1:])
    return (moe_out, kv_cache)


def solution(mesh):
    in_specs = (
        P(("dp", "expert"), None),
        P(),
        P(),
        P("expert", None, "dp"),
        P("expert", None, "dp"),
        P("expert", "dp", None),
        P("dp", None, None),
        P(),
        P(None, "expert", None, None, None),
    )
    out_specs = (P(("dp", "expert"), None), P("dp", "expert", None, None, None))
    return jax.shard_map(local, mesh=mesh, in_specs=in_specs, out_specs=out_specs, check_vma=False)
```

profile of v0, /device:TPU:1, one launch (start us, length us, event | category | flops | bytes accessed | tf_op | source)
XLA Modules:
  0.0 272.8 jit_solution(7578797608724495571)
XLA Ops:
  7.2 0.0 copy-start
  7.2 1.3 fusion.28
  8.5 0.0 copy-start.5
  8.5 0.7 convert_element_type.51
  9.2 0.7 add_select_fusion
  9.9 0.7 broadcast_compare_fusion
  10.7 1.3 convert_reduce_fusion
  11.9 0.4 fusion.22
  12.3 0.0 copy-done.5
  12.3 2.4 convolution_convert_fusion.3
  14.8 8.6 %all-to-all-start = ((bf16[32,8,2048]{2,1,0:T(8,128)(2,1)}), bf16[32,8,2048]{2,1,0:T(8,128)(2,1)}, u32[]{:S(2)}, u32[]{:S(2)}) async-start(bf16[32,8,2048]{2,1,0:T(8,128)(2,1)} %convolution_convert_fusion.3), calls=%async_computation | async-start | bytes 2097152 | tf_op jit(solution)/shard_map/all_to_all | solution.py:60
  23.4 0.0 all-gather.3.cloned.1.call-start
  23.5 0.0 copy-start.4
  23.5 16.8 %all-to-all-done = bf16[32,8,2048]{2,1,0:T(8,128)(2,1)} async-done(((bf16[32,8,2048]{2,1,0:T(8,128)(2,1)}), bf16[32,8,2048]{2,1,0:T(8,128)(2,1)}, u32[]{:S(2)}, u32[]{:S(2)}) %all-to-all-start) | async-done | bytes 1048608 | tf_op jit(solution)/shard_map/all_to_all | solution.py:60
  40.4 2.4 fusion.14
  42.7 0.0 all-gather.3.cloned.1.call-update
  42.8 0.0 reduce-scatter.2.cloned.1.call-start
  42.8 53.8 %all-gather.3.cloned.1.call-done = bf16[1024,2048]{1,0:T(8,128)(2,1)} async-done(((bf16[128,2048]{1,0:T(8,128)(2,1)}), bf16[1024,2048]{1,0:T(8,128)(2,1)}) %all-gather.3.cloned.1.call-update) | async-done | bytes 4194320 | tf_op jit(solution)/shard_map/all_gather | solution.py:67
  96.6 7.9 %fusion.10 = f32[1024,640]{1,0:T(8,128)} fusion(bf16[1024,2048]{1,0:T(8,128)(2,1)} %all-gather.3.cloned.1.call-done, bf16[1,2048,640]{2,1,0:T(8,128)(2,1)} %param.13), kind=kOutput, calls=%fused_computation.13 | convolution fusion | flops 2684354560 | bytes 9437184 | tf_op jit(solution)/shard_map/dot_general | solution.py:69
  104.5 0.0 copy-done.4
  104.5 12.8 %convolution_convert_fusion = bf16[1024,2048]{1,0:T(8,128)(2,1)} fusion(bf16[1,640,2048]{2,1,0:T(8,128)(2,1)} %param.14, f32[1024,640]{1,0:T(8,128)} %fusion.10, bf16[1024,2048]{1,0:T(8,128)(2,1)} %all-gather.3.cloned.1.call-done, bf16[1,2048,640]{2,1,0:T(8,128)(2,1)} %param.12), kind=kOutput, calls=%fused_computation.1 | convolution fusion | flops 5377359872 | bytes 16252928 | tf_op jit(solution)/shard_map/dot_general | solution.py:72
  117.4 0.0 reduce-scatter.2.cloned.1.call-update
  117.4 0.0 copy-start.3
  117.4 0.0 copy-start.1
  117.4 54.2 %reduce-scatter.2.cloned.1.call-done = bf16[128,2048]{1,0:T(8,128)(2,1)} async-done(((bf16[1024,2048]{1,0:T(8,128)(2,1)}), bf16[128,2048]{1,0:T(8,128)(2,1)}) %reduce-scatter.2.cloned.1.call-update) | async-done | bytes 524304 | tf_op jit(solution)/shard_map/reduce_scatter | solution.py:71
  171.6 2.5 convolution_convert_fusion.2
  174.0 7.6 %all-to-all-start.1 = ((bf16[32,8,2048]{2,1,0:T(8,128)(2,1)}), bf16[32,8,2048]{2,1,0:T(8,128)(2,1)}, u32[]{:S(2)}, u32[]{:S(2)}) async-start(bf16[32,8,2048]{2,1,0:T(8,128)(2,1)} %convolution_convert_fusion.2), calls=%async_computation.2 | async-start | bytes 2097152 | tf_op jit(solution)/shard_map/all_to_all | solution.py:80
  181.7 0.2 all-gather.5.cloned.1.call-start
  181.9 0.0 copy-done.3
  181.9 0.6 convert_element_type.61
  182.5 0.0 copy-done.1
  182.5 1.8 fusion.21
  184.3 14.3 %all-to-all-done.1 = bf16[32,8,2048]{2,1,0:T(8,128)(2,1)} async-done(((bf16[32,8,2048]{2,1,0:T(8,128)(2,1)}), bf16[32,8,2048]{2,1,0:T(8,128)(2,1)}, u32[]{:S(2)}, u32[]{:S(2)}) %all-to-all-start.1) | async-done | bytes 1048608 | tf_op jit(solution)/shard_map/all_to_all | solution.py:80
  198.6 1.7 fusion.25
  200.3 0.0 copy-start.2
  200.4 0.7 copy-done.2
  201.0 1.5 fusion.27
  202.6 0.0 all-gather.5.cloned.1.call-update
  202.6 53.4 %all-gather.5.cloned.1.call-done = bf16[2048,2048]{1,0:T(8,128)(2,1)} async-done(((bf16[64,2048]{1,0:T(8,128)(2,1)}), bf16[2048,2048]{1,0:T(8,128)(2,1)}) %all-gather.5.cloned.1.call-update) | async-done | bytes 8388624 | tf_op jit(solution)/shard_map/all_gather | solution.py:87
  256.0 0.0 copy-done
  256.0 10.2 %convolution_convert_fusion.1 = bf16[2048,768]{0,1:T(8,128)(2,1)} fusion(bf16[2048,2048]{1,0:T(8,128)(2,1)} %all-gather.5.cloned.1.call-done, bf16[2048,768]{0,1:T(8,128)(2,1)S(1)} %bitcast.74), kind=kOutput, calls=%fused_computation.2 | convolution fusion | flops 6444023808 | bytes 14680064 | tf_op jit(solution)/shard_map/dot_general | solution.py:86
  (6 shorter events, 0.1 us)
Async XLA Ops:
  7.2 248.8 %copy-start = (bf16[2048,1,6,2,64]{0,4,3,2,1:T(8,128)(2,1)S(1)}, bf16[2048,1,6,2,64]{0,4,3,2,1:T(8,128)(2,1)}, u32[]{:S(2)}) copy-start(bf16[2048,1,6,2,64]{0,4,3,2,1:T(8,128)(2,1)} %param.17) | copy-start | bytes 9437188
  8.5 3.8 %copy-start.5 = (f32[64]{0:T(128)}, f32[64]{0:T(128)S(1)}, u32[]{:S(2)}) copy-start(f32[64]{0:T(128)S(1)} %add_rsqrt_fusion.1) | copy-start | bytes 772
  14.8 25.6 %all-to-all-start = ((bf16[32,8,2048]{2,1,0:T(8,128)(2,1)}), bf16[32,8,2048]{2,1,0:T(8,128)(2,1)}, u32[]{:S(2)}, u32[]{:S(2)}) async-start(bf16[32,8,2048]{2,1,0:T(8,128)(2,1)} %convolution_convert_fusion.3), calls=%async_computation | async-start | bytes 2097152 | tf_op jit(solution)/shard_map/all_to_all | solution.py:60
  23.4 73.2 %all-gather.3.cloned.1.call-start = ((), (), s32[]{:S(2)}) async-start(), calls=%async_computation.3 | async-start | bytes 4718592 | tf_op jit(solution)/shard_map/all_gather | solution.py:67
  23.5 81.1 %copy-start.4 = (pred[128,8]{0,1:T(8,128)(4,1)}, pred[128,8]{0,1:T(8,128)(4,1)S(1)}, u32[]{:S(2)}) copy-start(pred[128,8]{0,1:T(8,128)(4,1)S(1)} %iota_compare_fusion.5) | copy-start | bytes 3076
  42.8 128.8 %reduce-scatter.2.cloned.1.call-start = ((), (), s32[]{:S(2)}) async-start(), calls=%async_computation.4 | async-start | bytes 4718592 | tf_op jit(solution)/shard_map/reduce_scatter | solution.py:71
  117.4 64.5 %copy-start.3 = (bf16[2048]{0:T(1024)(128)(2,1)S(1)}, bf16[2048]{0:T(1024)(128)(2,1)}, u32[]{:S(2)}) copy-start(bf16[2048]{0:T(1024)(128)(2,1)} %param.16) | copy-start | bytes 12292
  117.4 65.1 %copy-start.1 = (bf16[64,2048]{1,0:T(8,128)(2,1)S(1)}, bf16[64,2048]{1,0:T(8,128)(2,1)}, u32[]{:S(2)}) copy-start(bf16[64,2048]{1,0:T(8,128)(2,1)} %param.9) | copy-start | bytes 786436
  174.0 24.6 %all-to-all-start.1 = ((bf16[32,8,2048]{2,1,0:T(8,128)(2,1)}), bf16[32,8,2048]{2,1,0:T(8,128)(2,1)}, u32[]{:S(2)}, u32[]{:S(2)}) async-start(bf16[32,8,2048]{2,1,0:T(8,128)(2,1)} %convolution_convert_fusion.2), calls=%async_computation.2 | async-start | bytes 2097152 | tf_op jit(solution)/shard_map/all_to_all | solution.py:80
  181.7 74.3 %all-gather.5.cloned.1.call-start = ((), (), s32[]{:S(2)}) async-start(), calls=%async_computation.5 | async-start | bytes 8650752 | tf_op jit(solution)/shard_map/all_gather | solution.py:87
  200.3 0.7 copy-start.2
Sparse Core Ops, SparseCore 0:
  42.9 53.7 all-gather.2
  117.5 54.0 reduce-scatter.1
  202.7 53.2 all-gather.4
where the time goes:
time: 273 us
  waiting for transfers between devices  193 us (71%)
  matrix products  42.1 us (15%)
  starting transfers between devices  16.6 us (6%)
  between operations  13.9 us (5%)
  other arithmetic  6.87 us (3%)
    reduce_scatter x1, waiting for transfers between devices, local(): lax.psum_scatter(jnp.dot(hidden_all, down_proj, preferred_element_type=jn...  54.2 us
    all_gather x1, waiting for transfers between devices, local(): block_rows = lax.all_gather(picked, 'dp', axis=0, tiled=True)  53.8 us
    all_gather x1, waiting for transfers between devices, local(): lax.all_gather(encoded, 'expert', axis=0, tiled=True)  53.4 us
    all_to_all x1, waiting for transfers between devices, local(): lax.all_to_all(outgoing, 'expert', split_axis=0, concat_axis=0, tiled=True)  16.8 us
    all_to_all x1, waiting for transfers between devices, local(): lax.all_to_all(outbound, 'expert', split_axis=0, concat_axis=0, tiled=True)  14.3 us
    dot_general x1, matrix products, local(): jnp.dot(hidden_all, down_proj, preferred_element_type=jnp.float32)  12.8 us
    dot_general x1, matrix products, local(): jnp.dot(lax.all_gather(encoded, 'expert', axis=0, tiled=True), kv_matrix,...  10.2 us
    all_to_all x1, starting transfers between devices, local(): lax.all_to_all(outgoing, 'expert', split_axis=0, concat_axis=0, tiled=True)  8.64 us
  transfers between devices with their start and end apart: 5, of which 5 were waited for; matrix products, arithmetic and copies ran while one was open for 1% of the time, Pallas kernels for 0%

commit v1 on v0

--- a/solution.py
+++ b/solution.py
@@ -1,7 +1,158 @@
 import jax
 import jax.numpy as jnp
 from jax import lax
+from jax.experimental import pallas as pl
+from jax.experimental.pallas import tpu as pltpu
 from jax.sharding import PartitionSpec as P
+
+MESH = pl.DeviceIdType.MESH
+PLACE = {0: 0, 1: 1, 7: 2, 2: 3, 6: 4, 3: 5, 5: 6, 4: 7}
+RS_RIGHT = ((3, 1), (4, 0), (2, 1), (3, 0), (1, 1), (2, 0), (1, 0))
+RS_LEFT = tuple(((8 - r) % 8, 1 - h) for r, h in RS_RIGHT)
+
+
+def ring_kernel(picked, gate_w, up_w, down_w, out, wgu, wdn, rows, hid, part, landed,
+                w_sem, own_sem, ag_send, ag_recv, rs_send, rs_recv):
+    me = lax.axis_index("dp")
+    n = lax.axis_size("dp")
+    right = lax.rem(me + 1, n)
+    left = lax.rem(me + n - 1, n)
+    half = picked.shape[0] // 2
+    blk = 2 * half
+    tiles = wgu.shape[0]
+    lanes = wgu.shape[2] // 2
+
+    loads = []
+    for j in range(tiles):
+        cols = pl.ds(j * lanes, lanes)
+        loads.append(pltpu.make_async_copy(gate_w.at[0, :, cols], wgu.at[j, :, pl.ds(0, lanes)], w_sem.at[2 * j]))
+        loads.append(pltpu.make_async_copy(up_w.at[0, :, cols], wgu.at[j, :, pl.ds(lanes, lanes)], w_sem.at[2 * j + 1]))
+    loads.append(pltpu.make_async_copy(down_w.at[0], wdn, w_sem.at[2 * tiles]))
+    own = pltpu.make_async_copy(picked, rows.at[pl.ds(0, blk)], own_sem)
+    own.start()
+    for c in loads:
+        c.start()
+
+    barrier = pltpu.get_barrier_semaphore()
+    for nb in (left, right):
+        pl.semaphore_signal(barrier, inc=1, device_id={"dp": nb}, device_id_type=MESH)
+    pl.semaphore_wait(barrier, 2)
+    own.wait()
+
+    def rows_at(r, h):
+        return pl.ds(PLACE[r] * blk + h * half, half)
+
+    def ag_copy(d, i):
+        k = i // 2
+        if d == 0:
+            h = i % 2
+            src, dst = (8 - k) % 8, (7 - k) % 8
+        else:
+            h = 1 - i % 2
+            src, dst = k, k + 1
+        return pltpu.make_async_remote_copy(
+            src_ref=rows.at[rows_at(src, h)], dst_ref=rows.at[rows_at(dst, h)],
+            send_sem=ag_send.at[d, i], recv_sem=ag_recv.at[d, i],
+            device_id={"dp": (right, left)[d]}, device_id_type=MESH)
+
+    ag = [[ag_copy(d, i) for i in range(7)] for d in range(2)]
+
+    def rs_copy(d, i):
+        r, h = (RS_RIGHT, RS_LEFT)[d][i]
+        return pltpu.make_async_remote_copy(
+            src_ref=part.at[rows_at(r, h)], dst_ref=landed.at[d, i],
+            send_sem=rs_send.at[d, i], recv_sem=rs_recv.at[d, i],
+            device_id={"dp": (right, left)[d]}, device_id_type=MESH)
+
+    rs = [[rs_copy(d, i) for i in range(7)] for d in range(2)]
+
+    def ffn(start, m):
+        x = rows[pl.ds(start, m), :]
+        for j in range(tiles):
+            acc = jnp.dot(x, wgu[j], preferred_element_type=jnp.float32)
+            hid[pl.ds(0, m), pl.ds(j * lanes, lanes)] = (
+                jax.nn.gelu(acc[:, :lanes], approximate=True) * acc[:, lanes:]
+            ).astype(jnp.bfloat16)
+        width = wdn.shape[1] // 4
+        for j in range(4):
+            cols = pl.ds(j * width, width)
+            part[pl.ds(start, m), cols] = jnp.dot(
+                hid[pl.ds(0, m), :], wdn[:, cols], preferred_element_type=jnp.float32
+            ).astype(jnp.bfloat16)
+
+    for i in range(2):
+        for d in range(2):
+            ag[d][i].start()
+    for c in loads:
+        c.wait()
+    ffn(0, blk)
+    for k in range(1, 4):
+        for i in (2 * k - 2, 2 * k - 1):
+            for d in range(2):
+                ag[d][i].wait_recv()
+                if i + 2 < 7:
+                    ag[d][i + 2].start()
+        ffn(blk + 2 * blk * (k - 1), 2 * blk)
+    for d in range(2):
+        rs[d][0].start()
+    for d in range(2):
+        ag[d][6].wait_recv()
+    ffn(7 * blk, blk)
+    for d in range(2):
+        rs[d][1].start()
+    for i in range(7):
+        for d in range(2):
+            rs[d][i].wait_recv()
+            order = (RS_RIGHT, RS_LEFT)[d]
+            r, h = order[i]
+            r = (r - 1 + 2 * d) % 8
+            if r == 0:
+                continue
+            at = rows_at(r, h)
+            part[at, :] = (part[at, :].astype(jnp.float32) + landed[d, i].astype(jnp.float32)).astype(jnp.bfloat16)
+            rs[d][order.index((r, h))].start()
+    for h in range(2):
+        at = pl.ds(h * half, half)
+        total = part[at, :].astype(jnp.float32)
+        for d in range(2):
+            i = 6 if d == h else 4
+            total = total + landed[d, i].astype(jnp.float32)
+        out[at, :] = total.astype(jnp.bfloat16)
+    for d in range(2):
+        for i in range(7):
+            ag[d][i].wait_send()
+            rs[d][i].wait_send()
+
+
+def expert_ffn(picked, gate_weight, up_weight, down_weight):
+    blk, dim = picked.shape
+    ff = gate_weight.shape[2]
+    lanes = 128
+    tiles = ff // lanes
+    return pl.pallas_call(
+        ring_kernel,
+        out_shape=jax.ShapeDtypeStruct((blk, dim), jnp.bfloat16),
+        in_specs=[pl.BlockSpec(memory_space=pl.ANY)] * 4,
+        out_specs=pl.BlockSpec(memory_space=pltpu.VMEM),
+        scratch_shapes=[
+            pltpu.VMEM((tiles, dim, 2 * lanes), jnp.bfloat16),
+            pltpu.VMEM((ff, dim), jnp.bfloat16),
+            pltpu.VMEM((8 * blk, dim), jnp.bfloat16),
+            pltpu.VMEM((2 * blk, ff), jnp.bfloat16),
+            pltpu.VMEM((8 * blk, dim), jnp.bfloat16),
+            pltpu.VMEM((2, 7, blk // 2, dim), jnp.bfloat16),
+            pltpu.SemaphoreType.DMA((2 * tiles + 1,)),
+            pltpu.SemaphoreType.DMA,
+            pltpu.SemaphoreType.DMA((2, 7)),
+            pltpu.SemaphoreType.DMA((2, 7)),
+            pltpu.SemaphoreType.DMA((2, 7)),
+            pltpu.SemaphoreType.DMA((2, 7)),
+        ],
+        compiler_params=pltpu.CompilerParams(
+            collective_id=0, has_side_effects=True, vmem_limit_bytes=60 * 1024 * 1024
+        ),
+        name="ring_ffn",
+    )(picked, gate_weight, up_weight, down_weight)
 
 
 def normalize(values, gain):
@@ -61,19 +212,7 @@
     picked = jnp.einsum(
         "csm,smd->cd", compact_map, incoming, preferred_element_type=jnp.float32
     ).astype(jnp.bfloat16)
-    gate_proj = gate_weight[0]
-    up_proj = up_weight[0]
-    down_proj = down_weight[0]
-    block_rows = lax.all_gather(picked, "dp", axis=0, tiled=True)
-    gate_act = jnp.dot(block_rows, gate_proj, preferred_element_type=jnp.float32)
-    up_act = jnp.dot(block_rows, up_proj, preferred_element_type=jnp.float32)
-    hidden_all = (jax.nn.gelu(gate_act, approximate=True) * up_act).astype(jnp.bfloat16)
-    summed = lax.psum_scatter(
-        jnp.dot(hidden_all, down_proj, preferred_element_type=jnp.float32).astype(jnp.bfloat16),
-        "dp",
-        scatter_dimension=0,
-        tiled=True,
-    )
+    summed = expert_ffn(picked, gate_weight, up_weight, down_weight)
     outbound = jnp.einsum(
         "csm,cd->smd", compact_map, summed, preferred_element_type=jnp.float32
     ).astype(jnp.bfloat16)

time: 273 us -> 232 us (0.85)
  waiting for transfers between devices: 193 us -> 83.9 us
  Pallas kernels: 0 us -> 90.7 us
  matrix products: 42.1 us -> 21.4 us
    pallas_call x0 -> x1, Pallas kernels: none -> 90.7 us  [expert_ffn(): pl.pallas_call(ring_kernel, out_shape=jax.ShapeDtypeStruct((blk, dim), jn...]
    reduce_scatter x1 -> x0, waiting for transfers between devices: 54.2 us -> none  [local(): lax.psum_scatter(jnp.dot(hidden_all, down_proj, preferred_element_type=jn...]
    all_gather x1 -> x0, waiting for transfers between devices: 53.8 us -> none  [local(): block_rows = lax.all_gather(picked, 'dp', axis=0, tiled=True)]
    dot_general x2 -> x0, matrix products: 20.8 us -> none  [the longest x1 12.8 us: local(): jnp.dot(hidden_all, down_proj, preferred_element_type=jnp.float32)]
  transfers between devices with their start and end apart: 5 -> 3, of which waited for: 5 -> 3; matrix products, arithmetic and copies ran while one was open for 1% -> 1% of each run, Pallas kernels for 0% -> 0%
where the time goes in v1:
time: 232 us
  Pallas kernels  90.7 us (39%)
  waiting for transfers between devices  83.9 us (36%)
  matrix products  21.4 us (9%)
  starting transfers between devices  14.4 us (6%)
  between operations  14.2 us (6%)
  other arithmetic  6.27 us (3%)
    pallas_call x1, Pallas kernels, expert_ffn(): pl.pallas_call(ring_kernel, out_shape=jax.ShapeDtypeStruct((blk, dim), jn...  90.7 us
    all_gather x1, waiting for transfers between devices, local(): lax.all_gather(encoded, 'expert', axis=0, tiled=True)  52.7 us
    all_to_all x1, waiting for transfers between devices, local(): lax.all_to_all(outgoing, 'expert', split_axis=0, concat_axis=0, tiled=True)  16.9 us
    all_to_all x1, waiting for transfers between devices, local(): lax.all_to_all(outbound, 'expert', split_axis=0, concat_axis=0, tiled=True)  14.3 us
    dot_general x1, matrix products, local(): jnp.dot(lax.all_gather(encoded, 'expert', axis=0, tiled=True), kv_matrix,...  10.2 us
    all_to_all x1, starting transfers between devices, local(): lax.all_to_all(outgoing, 'expert', split_axis=0, concat_axis=0, tiled=True)  8.63 us
    all_to_all x1, starting transfers between devices, local(): lax.all_to_all(outbound, 'expert', split_axis=0, concat_axis=0, tiled=True)  5.51 us
  transfers between devices with their start and end apart: 3, of which 3 were waited for; matrix products, arithmetic and copies ran while one was open for 1% of the time, Pallas kernels for 0%

profile of v1, /device:TPU:1, one launch (start us, length us, event | category | flops | bytes accessed | tf_op | source)
XLA Modules:
  0.0 231.6 jit_solution(6102437868661018308)
XLA Ops:
  7.2 0.0 copy-start
  7.2 1.3 fusion.10
  8.5 0.0 copy-start.3
  8.5 0.7 convert_element_type.45
  9.2 0.7 add_select_fusion
  9.9 0.7 broadcast_compare_fusion
  10.7 1.3 convert_reduce_fusion
  11.9 0.4 fusion.6
  12.3 0.0 copy-done.3
  12.3 2.4 %convolution_convert_fusion.2 = bf16[32,8,2048]{2,1,0:T(8,128)(2,1)} fusion(bf16[64,2048]{1,0:T(8,128)(2,1)} %param.9, f32[2048]{0:T(1024)S(1)} %convert_element_type.45, f32[64]{0:T(128)S(1)} %add_rsqrt_fusion.1, f32[32,8,64]{2,1,0:T(8,128)S(1)} %fusion.6), kind=kOutput, calls=%fused_computation.2 | convolution fusion | flops 68173824 | bytes 1384704 | tf_op jit(solution)/shard_map/emt,td->emd/dot_general | solution.py:208
  14.8 8.6 %all-to-all-start = ((bf16[32,8,2048]{2,1,0:T(8,128)(2,1)}), bf16[32,8,2048]{2,1,0:T(8,128)(2,1)}, u32[]{:S(2)}, u32[]{:S(2)}) async-start(bf16[32,8,2048]{2,1,0:T(8,128)(2,1)} %convolution_convert_fusion.2), calls=%async_computation | async-start | bytes 2097152 | tf_op jit(solution)/shard_map/all_to_all | solution.py:211
  23.4 16.9 %all-to-all-done = bf16[32,8,2048]{2,1,0:T(8,128)(2,1)} async-done(((bf16[32,8,2048]{2,1,0:T(8,128)(2,1)}), bf16[32,8,2048]{2,1,0:T(8,128)(2,1)}, u32[]{:S(2)}, u32[]{:S(2)}) %all-to-all-start) | async-done | bytes 1048608 | tf_op jit(solution)/shard_map/all_to_all | solution.py:211
  40.3 2.4 %fusion.picked = bf16[128,2048]{1,0:T(8,128)(2,1)} fusion(bf16[32,8,2048]{2,1,0:T(8,128)(2,1)} %all-to-all-done, pred[128,8]{0,1:T(8,128)(4,1)S(1)} %iota_compare_fusion.5, pred[128,32]{0,1:T(8,128)(4,1)S(1)} %iota_compare_fusion.4), kind=kOutput, calls=%fused_computation.4 | convolution fusion | flops 134512640 | bytes 1577984 | tf_op jit(solution)/shard_map/csm,smd->cd/dot_general | solution.py:212
  42.7 90.7 %ring_ffn.1 = bf16[128,2048]{1,0:T(8,128)(2,1)} custom-call(bf16[128,2048]{1,0:T(8,128)(2,1)} %fusion.picked, bf16[1,2048,640]{2,1,0:T(8,128)(2,1)} %gate_w.1, bf16[1,2048,640]{2,1,0:T(8,128)(2,1)} %up_w.1, bf16[1,640,2048]{2,1,0:T(8,128)(2,1)} %down_w.1), custom_call_target="tpu_custom_call" | custom-call | tf_op jit(solution)/shard_map/ring_ffn/pallas_call | solution.py:132
  133.5 0.0 copy-start.1
  133.5 2.5 %convolution_convert_fusion.1 = bf16[32,8,2048]{2,1,0:T(8,128)(2,1)} fusion(bf16[128,2048]{1,0:T(8,128)(2,1)} %ring_ffn.1, pred[128,8]{0,1:T(8,128)(4,1)S(1)} %iota_compare_fusion.5, pred[128,32]{0,1:T(8,128)(4,1)S(1)} %iota_compare_fusion.4), kind=kOutput, calls=%fused_computation.1 | convolution fusion | flops 134774784 | bytes 1577984 | tf_op jit(solution)/shard_map/csm,cd->smd/dot_general | solution.py:216
  136.0 5.5 %all-to-all-start.1 = ((bf16[32,8,2048]{2,1,0:T(8,128)(2,1)}), bf16[32,8,2048]{2,1,0:T(8,128)(2,1)}, u32[]{:S(2)}, u32[]{:S(2)}) async-start(bf16[32,8,2048]{2,1,0:T(8,128)(2,1)} %convolution_convert_fusion.1), calls=%async_computation.1 | async-start | bytes 2097152 | tf_op jit(solution)/shard_map/all_to_all | solution.py:219
  141.5 0.2 all-gather.2.cloned.1.call-start
  141.7 0.7 convert_element_type.53
  142.4 0.0 copy-done.1
  142.4 1.8 fusion.5
  144.2 14.3 %all-to-all-done.1 = bf16[32,8,2048]{2,1,0:T(8,128)(2,1)} async-done(((bf16[32,8,2048]{2,1,0:T(8,128)(2,1)}), bf16[32,8,2048]{2,1,0:T(8,128)(2,1)}, u32[]{:S(2)}, u32[]{:S(2)}) %all-to-all-start.1) | async-done | bytes 1048608 | tf_op jit(solution)/shard_map/all_to_all | solution.py:219
  158.5 1.7 fusion.7
  160.2 0.0 copy-start.2
  160.3 0.7 copy-done.2
  160.9 0.8 fusion.9
  161.8 0.0 all-gather.2.cloned.1.call-update
  161.8 52.7 %all-gather.2.cloned.1.call-done = bf16[2048,2048]{1,0:T(8,128)(2,1)} async-done(((bf16[64,2048]{1,0:T(8,128)(2,1)}), bf16[2048,2048]{1,0:T(8,128)(2,1)}) %all-gather.2.cloned.1.call-update) | async-done | bytes 8388624 | tf_op jit(solution)/shard_map/all_gather | solution.py:226
  214.5 0.0 copy-done
  214.5 10.2 %convolution_convert_fusion = bf16[2048,768]{0,1:T(8,128)(2,1)} fusion(bf16[2048,2048]{1,0:T(8,128)(2,1)} %all-gather.2.cloned.1.call-done, bf16[2048,768]{0,1:T(8,128)(2,1)S(1)} %bitcast.59), kind=kOutput, calls=%fused_computation | convolution fusion | flops 6444023808 | bytes 14680064 | tf_op jit(solution)/shard_map/dot_general | solution.py:225
  (6 shorter events, 0.1 us)
Async XLA Ops:
  7.2 207.3 %copy-start = (bf16[2048,1,6,2,64]{0,4,3,2,1:T(8,128)(2,1)S(1)}, bf16[2048,1,6,2,64]{0,4,3,2,1:T(8,128)(2,1)}, u32[]{:S(2)}) copy-start(bf16[2048,1,6,2,64]{0,4,3,2,1:T(8,128)(2,1)} %param.17) | copy-start | bytes 9437188
  8.5 3.8 %copy-start.3 = (f32[64]{0:T(128)}, f32[64]{0:T(128)S(1)}, u32[]{:S(2)}) copy-start(f32[64]{0:T(128)S(1)} %add_rsqrt_fusion.1) | copy-start | bytes 772
  14.8 25.6 %all-to-all-start = ((bf16[32,8,2048]{2,1,0:T(8,128)(2,1)}), bf16[32,8,2048]{2,1,0:T(8,128)(2,1)}, u32[]{:S(2)}, u32[]{:S(2)}) async-start(bf16[32,8,2048]{2,1,0:T(8,128)(2,1)} %convolution_convert_fusion.2), calls=%async_computation | async-start | bytes 2097152 | tf_op jit(solution)/shard_map/all_to_all | solution.py:211
  133.5 8.9 %copy-start.1 = (bf16[64,2048]{1,0:T(8,128)(2,1)S(1)}, bf16[64,2048]{1,0:T(8,128)(2,1)}, u32[]{:S(2)}) copy-start(bf16[64,2048]{1,0:T(8,128)(2,1)} %param.9) | copy-start | bytes 786436
  136.0 22.6 %all-to-all-start.1 = ((bf16[32,8,2048]{2,1,0:T(8,128)(2,1)}), bf16[32,8,2048]{2,1,0:T(8,128)(2,1)}, u32[]{:S(2)}, u32[]{:S(2)}) async-start(bf16[32,8,2048]{2,1,0:T(8,128)(2,1)} %convolution_convert_fusion.1), calls=%async_computation.1 | async-start | bytes 2097152 | tf_op jit(solution)/shard_map/all_to_all | solution.py:219
  141.5 73.0 %all-gather.2.cloned.1.call-start = ((), (), s32[]{:S(2)}) async-start(), calls=%async_computation.2 | async-start | bytes 8650752 | tf_op jit(solution)/shard_map/all_gather | solution.py:226
  160.2 0.7 copy-start.2
Sparse Core Ops, SparseCore 0:
  161.9 52.5 all-gather.1

commit v2 on v1

--- a/solution.py
+++ b/solution.py
@@ -153,6 +153,197 @@
         ),
         name="ring_ffn",
     )(picked, gate_weight, up_weight, down_weight)
+
+
+SIDE = 4
+ORDER = (0, 3, 1, 2)
+
+
+def plane_kernel(encoded, kv_t, out, blocks, wkv, tile, in_sem, w_sem, out_sem,
+                 send_sem, recv_sem, sub_send, sub_recv, twin_send, twin_recv):
+    me = lax.axis_index("expert")
+    core = lax.rem(me, 2)
+    chip = lax.div(me, 2)
+    pos = (lax.div(chip, SIDE), lax.rem(chip, SIDE))
+    tok = encoded.shape[0]
+    half = tok // 2
+    sub = half // 2
+
+    def shift(v, by):
+        return lax.rem(v + by, SIDE)
+
+    def member(x, y, c):
+        return (x * SIDE + y) * 2 + c
+
+    def coords(h, first, second):
+        a, b = shift(pos[h], first), shift(pos[1 - h], second)
+        return (a, b) if h == 0 else (b, a)
+
+    def start_of(h, first, second, c):
+        x, y = coords(h, first, second)
+        return member(x, y, c) * tok + h * half
+
+    load_w = pltpu.make_async_copy(kv_t, wkv, w_sem)
+    own = pltpu.make_async_copy(encoded, blocks.at[pl.ds(me * tok, tok)], in_sem)
+    own.start()
+    load_w.start()
+    peers = [member(*coords(h, f, 0), core) for h in range(2) for f in (1, 3)]
+    twin = member(*pos, 1 - core)
+    barrier = pltpu.get_barrier_semaphore()
+    for p in peers + [twin]:
+        pl.semaphore_signal(barrier, inc=1, device_id={"expert": p}, device_id_type=MESH)
+    pl.semaphore_wait(barrier, 5)
+    own.wait()
+
+    started = []
+
+    def remote(rows, n, send, recv, target):
+        at = blocks.at[pl.ds(pl.multiple_of(rows, 16), n)]
+        return pltpu.make_async_remote_copy(
+            src_ref=at, dst_ref=at, send_sem=send, recv_sem=recv,
+            device_id={"expert": target}, device_id_type=MESH)
+
+    def go(c):
+        c.start()
+        started.append(c)
+
+    def along_first(h, first, by):
+        f = (first - by) % SIDE
+        go(remote(start_of(h, first, 0, core), half, send_sem.at[h, f, 0, 0], recv_sem.at[h, f, 0],
+                  member(*coords(h, by, 0), core)))
+
+    def sub_along_first(h, first, by, part):
+        go(remote(start_of(h, first, 0, core) + part * sub, sub, sub_send.at[h, part], sub_recv.at[h, part],
+                  member(*coords(h, by, 0), core)))
+
+    def along_second(h, first, second, by):
+        s = (second - by) % SIDE
+        go(remote(start_of(h, first, second, core), half, send_sem.at[h, first, s, 1], recv_sem.at[h, first, s],
+                  member(*coords(h, 0, by), core)))
+
+    def to_twin(h, first, second):
+        go(remote(start_of(h, first, second, core), half, twin_send.at[h, first, second],
+                  twin_recv.at[h, first, second], twin))
+
+    def arrived(h, first, second):
+        rows = start_of(h, first, second, core)
+        if (first, second) == (2, 0):
+            for part in range(2):
+                remote(rows + part * sub, sub, sub_send.at[h, part], sub_recv.at[h, part], twin).wait_recv()
+        else:
+            remote(rows, half, send_sem.at[h, 0, 0, 0], recv_sem.at[h, first, second], twin).wait_recv()
+
+    def twin_arrived(h, first, second):
+        remote(start_of(h, first, second, 1 - core), half, twin_send.at[h, first, second],
+               twin_recv.at[h, first, second], twin).wait_recv()
+
+    def chip_ready(dx, dy):
+        for h in range(2):
+            twin_arrived(h, *((dx, dy) if h == 0 else (dy, dx)))
+
+    stores = []
+
+    def project(*chips):
+        for dx, dy in chips:
+            chip_ready(dx, dy)
+        starts = [member(shift(pos[0], dx), shift(pos[1], dy), 0) * tok for dx, dy in chips]
+        slot = len(stores) // 2
+        x = jnp.concatenate([blocks[pl.ds(pl.multiple_of(s, 2 * tok), 2 * tok), :] for s in starts], axis=0)
+        y = lax.dot_general(wkv[...], x, (((1,), (1,)), ((), ())), preferred_element_type=jnp.float32)
+        tile[slot] = y.astype(jnp.bfloat16)
+        for i, s in enumerate(starts):
+            c = pltpu.make_async_copy(
+                tile.at[slot, :, pl.ds(i * 2 * tok, 2 * tok)],
+                out.at[:, pl.ds(pl.multiple_of(s, 2 * tok), 2 * tok)], out_sem.at[len(stores)])
+            c.start()
+            stores.append(c)
+
+    for h in range(2):
+        for by in (1, 3):
+            along_first(h, 0, by)
+    for h in range(2):
+        for by in (1, 3):
+            along_second(h, 0, 0, by)
+    for h in range(2):
+        to_twin(h, 0, 0)
+    load_w.wait()
+    for h in range(2):
+        for f in (3, 1):
+            arrived(h, f, 0)
+            sub_along_first(h, f, (4 - f) % 4, 0 if f == 3 else 1)
+            for by in (1, 3):
+                along_second(h, f, 0, by)
+            to_twin(h, f, 0)
+    for s in (3, 1):
+        for h in range(2):
+            arrived(h, 0, s)
+            if s == 3:
+                along_second(h, 0, 3, 1)
+            to_twin(h, 0, s)
+    project((0, 0), (3, 0))
+    for h in range(2):
+        arrived(h, 2, 0)
+        for by in (1, 3):
+            along_second(h, 2, 0, by)
+        to_twin(h, 2, 0)
+    project((1, 0), (0, 3))
+    for f in (3, 1):
+        for s in (3, 1):
+            for h in range(2):
+                arrived(h, f, s)
+                if (f, s) == (1, 3):
+                    along_second(h, 1, 3, 1)
+                if (f, s) == (3, 1):
+                    along_second(h, 3, 1, 3)
+                to_twin(h, f, s)
+        if f == 3:
+            project((0, 1), (3, 3))
+    project((1, 1), (1, 3))
+    for s in (3, 1):
+        for h in range(2):
+            arrived(h, 2, s)
+            if s == 1:
+                along_second(h, 2, 1, 3)
+            to_twin(h, 2, s)
+    for f, chips in ((0, ((3, 1), (2, 0))), (1, ((0, 2), (1, 2))), (3, ((2, 1), (3, 2))), (2, ((2, 3), (2, 2)))):
+        for h in range(2):
+            arrived(h, f, 2)
+            to_twin(h, f, 2)
+        project(*chips)
+    for c in stores:
+        c.wait()
+    for c in started:
+        c.wait_send()
+
+
+def kv_projection(encoded, kv_t):
+    tok, dim = encoded.shape
+    width = kv_t.shape[0]
+    count = 2 * SIDE * SIDE
+    return pl.pallas_call(
+        plane_kernel,
+        out_shape=jax.ShapeDtypeStruct((width, count * tok), jnp.bfloat16),
+        in_specs=[pl.BlockSpec(memory_space=pl.ANY)] * 2,
+        out_specs=pl.BlockSpec(memory_space=pl.ANY),
+        scratch_shapes=[
+            pltpu.VMEM((count * tok, dim), jnp.bfloat16),
+            pltpu.VMEM((width, dim), jnp.bfloat16),
+            pltpu.VMEM((8, width, 4 * tok), jnp.bfloat16),
+            pltpu.SemaphoreType.DMA,
+            pltpu.SemaphoreType.DMA,
+            pltpu.SemaphoreType.DMA((16,)),
+            pltpu.SemaphoreType.DMA((2, 4, 4, 2)),
+            pltpu.SemaphoreType.DMA((2, 4, 4)),
+            pltpu.SemaphoreType.DMA((2, 2)),
+            pltpu.SemaphoreType.DMA((2, 2)),
+            pltpu.SemaphoreType.DMA((2, 4, 4)),
+            pltpu.SemaphoreType.DMA((2, 4, 4)),
+        ],
+        compiler_params=pltpu.CompilerParams(
+            collective_id=1, has_side_effects=True, vmem_limit_bytes=60 * 1024 * 1024
+        ),
+        name="plane_kv",
+    )(encoded, kv_t)
 
 
 def normalize(values, gain):
@@ -221,13 +412,10 @@
     combined = jnp.einsum("tem,emd->td", combine_weight, returned.astype(jnp.float32))
     moe_out = (wide_tokens + combined).astype(jnp.bfloat16)
     encoded = normalize(moe_out.astype(jnp.float32), final_gain).astype(jnp.bfloat16)
-    kv_matrix = kv_weight.reshape(kv_weight.shape[0], -1)
-    kv_rows = jnp.dot(
-        lax.all_gather(encoded, "expert", axis=0, tiled=True),
-        kv_matrix,
-        preferred_element_type=jnp.float32,
-    ).astype(jnp.bfloat16)
-    kv_cache = kv_rows.reshape((kv_rows.shape[0],) + kv_weight.shape[1:])
+    heads = kv_weight.shape[1:]
+    kv_t = kv_weight.transpose(1, 2, 3, 4, 0).reshape(-1, kv_weight.shape[0])
+    kv_rows = kv_projection(encoded, kv_t)
+    kv_cache = kv_rows.reshape(heads + (kv_rows.shape[1],)).transpose(4, 0, 1, 2, 3)
     return (moe_out, kv_cache)
 
 

time: 232 us -> 196 us (0.84)
  waiting for transfers between devices: 83.9 us -> 33.5 us
  Pallas kernels: 90.7 us -> 131 us
  matrix products: 21.4 us -> 7.15 us
  between operations: 14.2 us -> 0.81 us
  local copies, waits for them, and re-layouts: 0.73 us -> 4.01 us
    all_gather x1 -> x0, waiting for transfers between devices: 52.7 us -> none  [local(): lax.all_gather(encoded, 'expert', axis=0, tiled=True)]
    pallas_call x0 -> x1, Pallas kernels: none -> 40.2 us  [kv_projection(): pl.pallas_call(plane_kernel, out_shape=jax.ShapeDtypeStruct((width, count...]
    dot_general x1 -> x0, matrix products: 10.2 us -> none  [local(): jnp.dot(lax.all_gather(encoded, 'expert', axis=0, tiled=True), kv_matrix,...]
    unnamed x8 -> x9, local copies, waits for them, and re-layouts: 0.71 us -> 4 us
    all_to_all x1, waiting for transfers between devices: 14.3 us -> 16.7 us  [local(): lax.all_to_all(outbound, 'expert', split_axis=0, concat_axis=0, tiled=True)]
  transfers between devices with their start and end apart: 3 -> 2, of which waited for: 3 -> 2; matrix products, arithmetic and copies ran while one was open for 1% -> 0% of each run, Pallas kernels for 0% -> 0%
where the time goes in v2:
time: 196 us; the launch traced here: 195 us
  Pallas kernels  131 us (67%)
  waiting for transfers between devices  33.5 us (17%)
  starting transfers between devices  13.4 us (7%)
  matrix products  7.15 us (4%)
  other arithmetic  5.47 us (3%)
  local copies, waits for them, and re-layouts  4.01 us (2%)
    pallas_call x1, Pallas kernels, expert_ffn(): pl.pallas_call(ring_kernel, out_shape=jax.ShapeDtypeStruct((blk, dim), jn...  90.7 us
    pallas_call x1, Pallas kernels, kv_projection(): pl.pallas_call(plane_kernel, out_shape=jax.ShapeDtypeStruct((width, count...  40.2 us
    all_to_all x1, waiting for transfers between devices, local(): lax.all_to_all(outgoing, 'expert', split_axis=0, concat_axis=0, tiled=True)  16.9 us
    all_to_all x1, waiting for transfers between devices, local(): lax.all_to_all(outbound, 'expert', split_axis=0, concat_axis=0, tiled=True)  16.7 us
    all_to_all x1, starting transfers between devices, local(): lax.all_to_all(outgoing, 'expert', split_axis=0, concat_axis=0, tiled=True)  8.59 us
    all_to_all x1, starting transfers between devices, local(): lax.all_to_all(outbound, 'expert', split_axis=0, concat_axis=0, tiled=True)  4.86 us
    unnamed x9, local copies, waits for them, and re-layouts  4 us
  transfers between devices with their start and end apart: 2, of which 2 were waited for; matrix products, arithmetic and copies ran while one was open for 0% of the time, Pallas kernels for 0%

profile of v2, /device:TPU:1, one launch (start us, length us, event | category | flops | bytes accessed | tf_op | source)
XLA Modules:
  0.0 195.3 jit_solution(7276541528105932097)
XLA Ops:
  0.6 0.0 copy-start
  0.7 1.1 fusion.10
  1.8 0.7 convert_element_type.42
  2.5 0.7 add_select_fusion
  3.3 0.7 broadcast_compare_fusion
  4.0 1.3 convert_reduce_fusion
  5.3 0.4 fusion.6
  5.7 2.4 %convolution_convert_fusion.1 = bf16[32,8,2048]{2,1,0:T(8,128)(2,1)} fusion(bf16[64,2048]{1,0:T(8,128)(2,1)} %param.9, f32[2048]{0:T(1024)S(1)} %convert_element_type.42, f32[64]{0:T(128)S(1)} %add_rsqrt_fusion.1, f32[32,8,64]{2,1,0:T(8,128)S(1)} %fusion.6), kind=kOutput, calls=%fused_computation.1 | convolution fusion | flops 68173824 | bytes 1384704 | tf_op jit(solution)/shard_map/emt,td->emd/dot_general | solution.py:399
  8.1 8.6 %all-to-all-start = ((bf16[32,8,2048]{2,1,0:T(8,128)(2,1)}), bf16[32,8,2048]{2,1,0:T(8,128)(2,1)S(1)}, u32[]{:S(2)}, u32[]{:S(2)}) async-start(bf16[32,8,2048]{2,1,0:T(8,128)(2,1)} %convolution_convert_fusion.1), calls=%async_computation | async-start | bytes 2097152 | tf_op jit(solution)/shard_map/all_to_all | solution.py:402
  16.7 16.9 %all-to-all-done = bf16[32,8,2048]{2,1,0:T(8,128)(2,1)S(1)} async-done(((bf16[32,8,2048]{2,1,0:T(8,128)(2,1)}), bf16[32,8,2048]{2,1,0:T(8,128)(2,1)S(1)}, u32[]{:S(2)}, u32[]{:S(2)}) %all-to-all-start) | async-done | bytes 1048608 | tf_op jit(solution)/shard_map/all_to_all | solution.py:402
  33.6 1.1 fusion.picked
  34.7 90.7 %ring_ffn.1 = bf16[128,2048]{1,0:T(8,128)(2,1)} custom-call(bf16[128,2048]{1,0:T(8,128)(2,1)} %fusion.picked, bf16[1,2048,640]{2,1,0:T(8,128)(2,1)} %gate_w.1, bf16[1,2048,640]{2,1,0:T(8,128)(2,1)} %up_w.1, bf16[1,640,2048]{2,1,0:T(8,128)(2,1)} %down_w.1), custom_call_target="tpu_custom_call" | custom-call | tf_op jit(solution)/shard_map/ring_ffn/pallas_call | solution.py:132
  125.5 0.0 copy-start.3
  125.5 0.0 copy-start.1
  125.5 2.5 %convolution_convert_fusion = bf16[32,8,2048]{2,1,0:T(8,128)(2,1)} fusion(bf16[128,2048]{1,0:T(8,128)(2,1)} %ring_ffn.1, pred[128,8]{0,1:T(8,128)(4,1)S(1)} %iota_compare_fusion.5, pred[128,32]{0,1:T(8,128)(4,1)S(1)} %iota_compare_fusion.4), kind=kOutput, calls=%fused_computation | convolution fusion | flops 134774784 | bytes 1577984 | tf_op jit(solution)/shard_map/csm,cd->smd/dot_general | solution.py:407
  128.0 4.9 %all-to-all-start.1 = ((bf16[32,8,2048]{2,1,0:T(8,128)(2,1)}), bf16[32,8,2048]{2,1,0:T(8,128)(2,1)S(1)}, u32[]{:S(2)}, u32[]{:S(2)}) async-start(bf16[32,8,2048]{2,1,0:T(8,128)(2,1)} %convolution_convert_fusion), calls=%async_computation.1 | async-start | bytes 2097152 | tf_op jit(solution)/shard_map/all_to_all | solution.py:410
  132.9 0.0 copy-done.3
  132.9 0.0 copy-done
  132.9 0.0 copy-done.1
  132.9 0.3 fusion.5
  133.2 16.7 %all-to-all-done.1 = bf16[32,8,2048]{2,1,0:T(8,128)(2,1)S(1)} async-done(((bf16[32,8,2048]{2,1,0:T(8,128)(2,1)}), bf16[32,8,2048]{2,1,0:T(8,128)(2,1)S(1)}, u32[]{:S(2)}, u32[]{:S(2)}) %all-to-all-start.1) | async-done | bytes 1048608 | tf_op jit(solution)/shard_map/all_to_all | solution.py:410
  149.9 0.4 fusion.7
  150.3 0.0 copy-start.2
  150.3 0.8 fusion.9.encoded
  151.1 40.2 %plane_kv.1 = bf16[768,2048]{1,0:T(8,128)(2,1)} custom-call(bf16[64,2048]{1,0:T(8,128)(2,1)} %fusion.9.encoded, bf16[768,2048]{1,0:T(8,128)(2,1)} %bitcast.62), custom_call_target="tpu_custom_call" | custom-call | tf_op jit(solution)/shard_map/plane_kv/pallas_call | solution.py:323
  191.4 0.0 copy-done.2
  191.4 4.0 %copy.15 = bf16[2048,1,6,2,64]{0,4,3,2,1:T(8,128)(2,1)} copy(bf16[2048,1,6,2,64]{0,4,3,2,1:T(8,128)(2,1)} %bitcast.61) | data formatting | bytes 6291456
  (7 shorter events, 0.1 us)
Async XLA Ops:
  0.6 132.2 %copy-start = (bf16[2048,32]{0,1:T(8,128)(2,1)S(1)}, bf16[2048,32]{0,1:T(8,128)(2,1)}, u32[]{:S(2)}) copy-start(bf16[2048,32]{0,1:T(8,128)(2,1)} %param.11) | copy-start | bytes 393220
  8.1 25.5 %all-to-all-start = ((bf16[32,8,2048]{2,1,0:T(8,128)(2,1)}), bf16[32,8,2048]{2,1,0:T(8,128)(2,1)S(1)}, u32[]{:S(2)}, u32[]{:S(2)}) async-start(bf16[32,8,2048]{2,1,0:T(8,128)(2,1)} %convolution_convert_fusion.1), calls=%async_computation | async-start | bytes 2097152 | tf_op jit(solution)/shard_map/all_to_all | solution.py:402
  125.5 7.4 %copy-start.3 = (bf16[2048]{0:T(1024)(128)(2,1)S(1)}, bf16[2048]{0:T(1024)(128)(2,1)}, u32[]{:S(2)}) copy-start(bf16[2048]{0:T(1024)(128)(2,1)} %param.16) | copy-start | bytes 12292
  125.5 7.4 %copy-start.1 = (bf16[64,2048]{1,0:T(8,128)(2,1)S(1)}, bf16[64,2048]{1,0:T(8,128)(2,1)}, u32[]{:S(2)}) copy-start(bf16[64,2048]{1,0:T(8,128)(2,1)} %param.9) | copy-start | bytes 786436
  128.0 21.9 %all-to-all-start.1 = ((bf16[32,8,2048]{2,1,0:T(8,128)(2,1)}), bf16[32,8,2048]{2,1,0:T(8,128)(2,1)S(1)}, u32[]{:S(2)}, u32[]{:S(2)}) async-start(bf16[32,8,2048]{2,1,0:T(8,128)(2,1)} %convolution_convert_fusion), calls=%async_computation.1 | async-start | bytes 2097152 | tf_op jit(solution)/shard_map/all_to_all | solution.py:410
  150.3 41.1 %copy-start.2 = (bf16[64,2048]{1,0:T(8,128)(2,1)}, bf16[64,2048]{1,0:T(8,128)(2,1)S(1)}, u32[]{:S(2)}) copy-start(bf16[64,2048]{1,0:T(8,128)(2,1)S(1)} %get-tuple-element.10) | copy-start | bytes 786436
